TPU v7x, 32 devices: a whole 2x2x4 slice. The times are simulated.
32 devices in a mesh: section: 2 (over core), row: 4 (over y, x), col: 4 (over z).
Axes of the slice: x: 2, y: 2, z: 4, core: 2. Of those that a mesh axis runs over, the one named last changes fastest.
Arguments:
- section_inputs: bfloat16 [2, 2, 48, 4096], P('section', None, 'col', 'row'), may hold values from -6 to 6
- out_grad: bfloat16 [2, 48, 4096], P(None, 'col', 'row'), may hold values from -6 to 6
- gate_weight: bfloat16 [2, 4096, 14336], P('section', 'row', 'col'), may hold values from -0.09375 to 0.09375
- up_weight: bfloat16 [2, 4096, 14336], P('section', 'row', 'col'), may hold values from -0.09375 to 0.09375
- down_weight: bfloat16 [2, 14336, 4096], P('section', 'col', 'row'), may hold values from -0.046875 to 0.046875
Outputs:
- input_grads: bfloat16 [2, 2, 48, 4096], P('section', None, 'col', 'row')
- grad_gate: float32 [2, 4096, 14336], P('section', 'row', 'col')
- grad_up: float32 [2, 4096, 14336], P('section', 'row', 'col')
- grad_down: float32 [2, 14336, 4096], P('section', 'col', 'row')
All inputs are finite; a program needn't handle non-finite values.
Results may differ from a plain program's by a relative error of at most 0.025.
Values may be sent and summed in bfloat16 or wider, within the bound.
A program may use at most 192 MiB of HBM per device.

v0:
```python
import jax
import jax.numpy as jnp
from jax import lax
from jax.sharding import PartitionSpec as P

CONTRACT_ROWS = (((0,), (0,)), ((), ()))
CONTRACT_COLS = (((1,), (1,)), ((), ()))


def passed_along(block, axis, distance):
    devices = range(lax.axis_size(axis))
    route = [(i - distance, i) for i in devices if i - distance in devices]
    return lax.ppermute(block, axis, route)


def spread_panel(panel):
    return lax.all_gather(panel, "col", axis=0, tiled=True)


def row_partials(make_terms, keep_rows):
    return lax.psum_scatter(
        make_terms(jnp.int32(0), keep_rows * lax.axis_size("row")).astype(jnp.bfloat16),
        "row",
        scatter_dimension=0,
        tiled=True,
    ).astype(jnp.float32)


def layer_backward(x_local, dy_local, w_both, w_down):
    hidden_width = w_down.shape[0]
    x_whole = spread_panel(x_local)
    dy_whole = spread_panel(dy_local)
    keep_rows = x_whole.shape[0] // lax.axis_size("row")

    def forward_terms(first_row, row_count):
        return jnp.dot(x_whole, w_both, preferred_element_type=jnp.float32)

    def backward_terms(first_row, row_count):
        return lax.dot_general(dy_whole, w_down, CONTRACT_COLS, preferred_element_type=jnp.float32)

    both_sums = row_partials(forward_terms, keep_rows)
    hidden_grad = row_partials(backward_terms, keep_rows)
    gate_sum = both_sums[:, :hidden_width]
    up_sum = both_sums[:, hidden_width:]
    sigmoid_gate = jax.nn.sigmoid(gate_sum)
    activated = gate_sum * sigmoid_gate
    slope = sigmoid_gate * (1.0 + gate_sum * (1.0 - sigmoid_gate))
    hidden = (activated * up_sum).astype(jnp.bfloat16)
    gate_grad = (hidden_grad * up_sum * slope).astype(jnp.bfloat16)
    up_grad = (hidden_grad * activated).astype(jnp.bfloat16)
    packed = jnp.concatenate([hidden, gate_grad, up_grad], axis=1)
    gathered = lax.all_gather(packed, "row", axis=0, tiled=True)
    hidden_whole = gathered[:, :hidden_width]
    both_grads = gathered[:, hidden_width:]
    branch_sum = lax.psum_scatter(
        lax.dot_general(
            both_grads, w_both, CONTRACT_COLS, preferred_element_type=jnp.float32
        ).astype(jnp.bfloat16),
        "col",
        scatter_dimension=0,
        tiled=True,
    ).astype(jnp.float32)
    input_grad = (dy_local.astype(jnp.float32) + branch_sum).astype(jnp.bfloat16)
    down_update = lax.dot_general(
        hidden_whole, dy_whole, CONTRACT_ROWS, preferred_element_type=jnp.float32
    )
    both_update = lax.dot_general(
        x_whole, both_grads, CONTRACT_ROWS, preferred_element_type=jnp.float32
    )
    return (input_grad, both_update, down_update)


def shards(section_inputs, out_grad, gate_weight, up_weight, down_weight):
    section_id = lax.axis_index("section")
    last_section = lax.axis_size("section") - 1
    is_last = section_id == last_section
    panels = section_inputs[0]
    w_both = jnp.concatenate([gate_weight[0], up_weight[0]], axis=1)
    w_down = down_weight[0]
    hidden_width = w_down.shape[0]
    micro_count = panels.shape[0]
    both_total = jnp.zeros(w_both.shape, jnp.float32)
    down_total = jnp.zeros(w_down.shape, jnp.float32)
    merged_shape = (micro_count * panels.shape[1], panels.shape[2])
    x_local = panels.reshape(merged_shape)
    top_grads = out_grad.reshape(merged_shape)
    received = jnp.zeros(merged_shape, jnp.bfloat16)
    merged_results = received
    for step_index in range(last_section + 1):
        is_active = section_id == last_section - step_index
        dy_local = jnp.where(is_last, top_grads, received)
        input_grad, both_update, down_update = layer_backward(x_local, dy_local, w_both, w_down)
        merged_results = jnp.where(is_active, input_grad, merged_results)
        both_total = both_total + jnp.where(is_active, both_update, 0.0)
        down_total = down_total + jnp.where(is_active, down_update, 0.0)
        if step_index < last_section:
            received = passed_along(input_grad, "section", -1)
    results = merged_results.reshape(panels.shape)
    return (
        results[None],
        both_total[:, :hidden_width][None],
        both_total[:, hidden_width:][None],
        down_total[None],
    )


def solution(mesh):
    return jax.shard_map(
        shards,
        mesh=mesh,
        in_specs=(
            P("section", None, "col", "row"),
            P(None, "col", "row"),
            P("section", "row", "col"),
            P("section", "row", "col"),
            P("section", "col", "row"),
        ),
        out_specs=(
            P("section", None, "col", "row"),
            P("section", "row", "col"),
            P("section", "row", "col"),
            P("section", "col", "row"),
        ),
        check_vma=False,
    )
```

profile of v0, /device:TPU:1, one launch (start us, length us, event | category | flops | bytes accessed | tf_op | source)
XLA Modules:
  0.0 341.2 jit_solution(15055987035588454683)
XLA Ops:
  8.0 12.8 %all_gather.16 = bf16[96,1024]{1,0:T(8,128)(2,1)S(1)} all-gather(bf16[24,1024]{1,0:T(8,128)(2,1)S(1)} %reshape_squeeze.3), channel_id=1, replica_groups=mesh['section'=2,'row'=4,'col'=4] {'col'}, dimensions={0}, use_global_device_ids=true | all-gather | bytes 245760 | tf_op jit(solution)/shard_map/all_gather | solution.py:17
  20.9 7.8 %fusion = bf16[96,7168]{1,0:T(8,128)(2,1)} fusion(bf16[96,1024]{1,0:T(8,128)(2,1)S(1)} %all_gather.16, bf16[1024,3584]{1,0:T(8,128)(2,1)} %bitcast.29, bf16[1024,3584]{1,0:T(8,128)(2,1)} %bitcast.32), kind=kOutput, calls=%fused_computation.6 | convolution fusion | flops 1439334400 | bytes 16252928 | tf_op jit(solution)/shard_map/dot_general | solution.py:36
  28.9 10.7 %all_gather.17 = bf16[96,1024]{1,0:T(8,128)(2,1)S(1)} all-gather(bf16[24,1024]{1,0:T(8,128)(2,1)S(1)} %broadcast_select_fusion.1), channel_id=1, replica_groups=mesh['section'=2,'row'=4,'col'=4] {'col'}, dimensions={0}, use_global_device_ids=true | all-gather | bytes 245760 | tf_op jit(solution)/shard_map/all_gather | solution.py:17
  39.5 6.3 %fusion.5 = bf16[96,3584]{1,0:T(8,128)(2,1)} fusion(bf16[96,1024]{1,0:T(8,128)(2,1)S(1)} %all_gather.17, bf16[1,3584,1024]{2,1,0:T(8,128)(2,1)} %param.9), kind=kOutput, calls=%fused_computation.11 | convolution fusion | flops 704987136 | bytes 8224768 | tf_op jit(solution)/shard_map/dot_general | solution.py:39
  45.9 15.9 %reduce-scatter.16.cloned.1.call-done = bf16[24,7168]{1,0:T(8,128)(2,1)} async-done(((bf16[96,7168]{1,0:T(8,128)(2,1)}), bf16[24,7168]{1,0:T(8,128)(2,1)}) %reduce-scatter.16.cloned.1.call-update) | async-done | bytes 344080
  62.8 28.2 %reduce-scatter.18.cloned.1.call-done = bf16[24,3584]{1,0:T(8,128)(2,1)} async-done(((bf16[96,3584]{1,0:T(8,128)(2,1)}), bf16[24,3584]{1,0:T(8,128)(2,1)}) %reduce-scatter.18.cloned.1.call-update) | async-done | bytes 172048
  91.1 1.1 fusion.30
  93.1 35.4 %all-gather.3.cloned.1.call-done = bf16[96,10752]{1,0:T(8,128)(2,1)} async-done(((bf16[24,10752]{1,0:T(8,128)(2,1)}), bf16[96,10752]{1,0:T(8,128)(2,1)}) %all-gather.3.cloned.1.call-update) | async-done | bytes 2064400 | tf_op jit(solution)/shard_map/all_gather | solution.py:52
  128.5 8.9 %fusion.18 = bf16[96,1024]{1,0:T(8,128)(2,1)} fusion(bf16[1024,3584]{1,0:T(8,128)(2,1)} %bitcast.30, bf16[1024,3584]{1,0:T(8,128)(2,1)} %bitcast.33, bf16[96,10752]{1,0:T(8,128)(2,1)} %all-gather.3.cloned.1.call-done), kind=kOutput, calls=%fused_computation.20 | convolution fusion | flops 1438744576 | bytes 16252928 | tf_op jit(solution)/shard_map/dot_general | solution.py:56
  137.5 17.5 %reduce-scatter.12.cloned.1.call-done = bf16[24,1024]{1,0:T(8,128)(2,1)} async-done(((bf16[96,1024]{1,0:T(8,128)(2,1)}), bf16[24,1024]{1,0:T(8,128)(2,1)}) %reduce-scatter.12.cloned.1.call-update) | async-done | bytes 49168 | tf_op jit(solution)/shard_map/reduce_scatter | solution.py:55
  155.8 5.0 %collective-permute-start = (bf16[24,1024]{1,0:T(8,128)(2,1)S(1)}, bf16[24,1024]{1,0:T(8,128)(2,1)S(1)}, u32[]{:S(2)}, u32[]{:S(2)}) collective-permute-start(bf16[24,1024]{1,0:T(8,128)(2,1)S(1)} %add_convert_fusion.1), channel_id=1, source_target_pairs={{16,0},{17,1},{18,2},{19,3},{20,4},{21,5},{22,6},{23,7},{24,8},{25... | collective-permute-start | bytes 147464 | tf_op jit(solution)/shard_map/ppermute | solution.py:13
  162.3 10.8 %all_gather.19 = bf16[96,1024]{1,0:T(8,128)(2,1)S(1)} all-gather(bf16[24,1024]{1,0:T(8,128)(2,1)S(1)} %broadcast_select_fusion), channel_id=1, replica_groups=mesh['section'=2,'row'=4,'col'=4] {'col'}, dimensions={0}, use_global_device_ids=true | all-gather | bytes 245760 | tf_op jit(solution)/shard_map/all_gather | solution.py:17
  173.0 6.3 %fusion.8 = bf16[96,3584]{1,0:T(8,128)(2,1)} fusion(bf16[96,1024]{1,0:T(8,128)(2,1)S(1)} %all_gather.19, bf16[1,3584,1024]{2,1,0:T(8,128)(2,1)} %param.9), kind=kOutput, calls=%fused_computation.12 | convolution fusion | flops 704987136 | bytes 8224768 | tf_op jit(solution)/shard_map/dot_general | solution.py:39
  179.4 26.7 %reduce-scatter.20.cloned.1.call-done = bf16[24,3584]{1,0:T(8,128)(2,1)} async-done(((bf16[96,3584]{1,0:T(8,128)(2,1)}), bf16[24,3584]{1,0:T(8,128)(2,1)}) %reduce-scatter.20.cloned.1.call-update) | async-done | bytes 172048
  206.1 1.1 fusion.33
  208.3 7.6 %fusion.25 = f32[3584,1024]{1,0:T(8,128)} fusion(bf16[96,1024]{1,0:T(8,128)(2,1)S(1)} %all_gather.17, bf16[96,10752]{1,0:T(8,128)(2,1)S(1)} %copy-done.1), kind=kOutput, calls=%fused_computation.23 | convolution fusion | flops 704643072 | bytes 15564800 | tf_op jit(solution)/shard_map/dot_general | solution.py:64
  215.9 11.6 %fusion.15 = f32[7168,1024]{1,0:T(8,128)} fusion(bf16[96,1024]{1,0:T(8,128)(2,1)S(1)} %all_gather.16, bf16[96,10752]{1,0:T(8,128)(2,1)S(1)} %copy-done.1), kind=kOutput, calls=%fused_computation.17 | convolution fusion | flops 1409286144 | bytes 30932992 | tf_op jit(solution)/shard_map/dot_general | solution.py:67
  227.5 15.9 %all-gather.5.cloned.1.call-done = bf16[96,10752]{1,0:T(8,128)(2,1)} async-done(((bf16[24,10752]{1,0:T(8,128)(2,1)}), bf16[96,10752]{1,0:T(8,128)(2,1)}) %all-gather.5.cloned.1.call-update) | async-done | bytes 2064400 | tf_op jit(solution)/shard_map/all_gather | solution.py:52
  243.4 9.0 %fusion.21 = bf16[96,1024]{1,0:T(8,128)(2,1)} fusion(bf16[1024,3584]{1,0:T(8,128)(2,1)} %bitcast.31, bf16[1024,3584]{1,0:T(8,128)(2,1)} %bitcast.34, bf16[96,10752]{1,0:T(8,128)(2,1)} %all-gather.5.cloned.1.call-done), kind=kOutput, calls=%fused_computation.21 | convolution fusion | flops 1438744576 | bytes 16252928 | tf_op jit(solution)/shard_map/dot_general | solution.py:56
  252.5 19.5 %add_bitcast_fusion = f32[1024,7168]{0,1:T(8,128)} fusion(f32[7168,1024]{1,0:T(8,128)} %fusion.15, pred[]{:T(512)S(6)} %eq.7, pred[]{:T(512)S(6)} %eq.8, bf16[96,1024]{1,0:T(8,128)(2,1)S(1)} %all_gather.16, bf16[96,10752]{1,0:T(8,128)(2,1)S(1)} %copy-done), kind=kOutput, calls=%fused_computation | convolution fusion | flops 1431306240 | bytes 60293120 | tf_op jit(solution)/shard_map/dot_general | solution.py:67
  271.9 19.6 %slice_bitcast_fusion = (f32[1,1024,3584]{1,2,0:T(8,128)}, f32[1,1024,3584]{1,2,0:T(8,128)}) fusion(f32[1024,7168]{0,1:T(8,128)} %add_bitcast_fusion), kind=kLoop, calls=%fused_computation.1 | loop fusion | bytes 58720256 | tf_op jit(solution)/shard_map/broadcast_in_dim | solution.py:102
  291.5 12.7 %add_bitcast_fusion.1 = f32[1,3584,1024]{2,1,0:T(8,128)} fusion(f32[3584,1024]{1,0:T(8,128)} %fusion.25, bf16[96,1024]{1,0:T(8,128)(2,1)S(1)} %all_gather.19, pred[]{:T(512)S(6)} %eq.7, pred[]{:T(512)S(6)} %eq.8, bf16[96,10752]{1,0:T(8,128)(2,1)S(1)} %copy-done), kind=kOutput, calls=%fused_computation.4 | convolution fusion | flops 715653120 | bytes 30244866 | tf_op jit(solution)/shard_map/dot_general | solution.py:64
  304.3 14.3 %copy.21 = f32[1,1024,3584]{2,1,0:T(8,128)} copy(f32[1,1024,3584]{1,2,0:T(8,128)} %get-tuple-element.17) | data formatting | bytes 29360128
  318.5 14.3 %copy.22 = f32[1,1024,3584]{2,1,0:T(8,128)} copy(f32[1,1024,3584]{1,2,0:T(8,128)} %get-tuple-element.16) | data formatting | bytes 29360128
  (43 shorter events, 8.0 us)
Async XLA Ops:
  7.2 54.6 %reduce-scatter.16.cloned.1.call-start = ((), (), s32[]{:S(2)}) async-start(), calls=%async_computation.9 | async-start | bytes 1720320
  20.9 7.9 %copy-start.6 = (bf16[2,12,1024]{2,0,1:T(2,128)(2,1)S(1)}, bf16[2,12,1024]{2,0,1:T(2,128)(2,1)}, u32[]{:S(2)}) copy-start(bf16[2,12,1024]{2,0,1:T(2,128)(2,1)} %param.6) | copy-start | bytes 147460
  28.7 62.3 %reduce-scatter.18.cloned.1.call-start = ((), (), s32[]{:S(2)}) async-start(), calls=%async_computation.10 | async-start | bytes 860160
  45.9 82.6 %all-gather.3.cloned.1.call-start = ((), (), s32[]{:S(2)}) async-start(), calls=%async_computation.5 | async-start | bytes 2580480 | tf_op jit(solution)/shard_map/all_gather | solution.py:52
  93.0 61.9 %reduce-scatter.12.cloned.1.call-start = ((), (), s32[]{:S(2)}) async-start(), calls=%async_computation.6 | async-start | bytes 245760 | tf_op jit(solution)/shard_map/reduce_scatter | solution.py:55
  137.4 70.9 %copy-start.1 = (bf16[96,10752]{1,0:T(8,128)(2,1)S(1)}, bf16[96,10752]{1,0:T(8,128)(2,1)}, u32[]{:S(2)}) copy-start(bf16[96,10752]{1,0:T(8,128)(2,1)} %all-gather.3.cloned.1.call-done) | copy-start | bytes 6193156
  137.4 68.7 %reduce-scatter.20.cloned.1.call-start = ((), (), s32[]{:S(2)}) async-start(), calls=%async_computation.11 | async-start | bytes 860160
  155.8 5.8 %copy-start.4 = (bf16[24,1024]{1,0:T(8,128)(2,1)}, bf16[24,1024]{1,0:T(8,128)(2,1)S(1)}, u32[]{:S(2)}) copy-start(bf16[24,1024]{1,0:T(8,128)(2,1)S(1)} %add_convert_fusion.1) | copy-start | bytes 147460
  155.8 5.8 %collective-permute-start = (bf16[24,1024]{1,0:T(8,128)(2,1)S(1)}, bf16[24,1024]{1,0:T(8,128)(2,1)S(1)}, u32[]{:S(2)}, u32[]{:S(2)}) collective-permute-start(bf16[24,1024]{1,0:T(8,128)(2,1)S(1)} %add_convert_fusion.1), channel_id=1, source_target_pairs={{16,0},{17,1},{18,2},{19,3},{20,4},{21,5},{22,6},{23,7},{24,8},{25... | collective-permute-start | bytes 147464 | tf_op jit(solution)/shard_map/ppermute | solution.py:13
  161.6 0.6 copy-start.2
  179.3 64.1 %all-gather.5.cloned.1.call-start = ((), (), s32[]{:S(2)}) async-start(), calls=%async_computation.7 | async-start | bytes 2580480 | tf_op jit(solution)/shard_map/all_gather | solution.py:52
  208.1 124.8 %reduce-scatter.14.cloned.1.call-start = ((), (), s32[]{:S(2)}) async-start(), calls=%async_computation.8 | async-start | bytes 245760 | tf_op jit(solution)/shard_map/reduce_scatter | solution.py:55
  243.4 9.1 %copy-start = (bf16[96,10752]{1,0:T(8,128)(2,1)S(1)}, bf16[96,10752]{1,0:T(8,128)(2,1)}, u32[]{:S(2)}) copy-start(bf16[96,10752]{1,0:T(8,128)(2,1)} %all-gather.5.cloned.1.call-done) | copy-start | bytes 6193156
  318.5 14.3 %copy-start.3 = (bf16[24,1024]{1,0:T(8,128)(2,1)S(1)}, bf16[24,1024]{1,0:T(8,128)(2,1)}, u32[]{:S(2)}) copy-start(bf16[24,1024]{1,0:T(8,128)(2,1)} %copy-done.2) | copy-start | bytes 147460
  318.5 14.3 %copy-start.5 = (bf16[24,1024]{1,0:T(8,128)(2,1)S(1)}, bf16[24,1024]{1,0:T(8,128)(2,1)}, u32[]{:S(2)}) copy-start(bf16[24,1024]{1,0:T(8,128)(2,1)} %copy-done.4) | copy-start | bytes 147460
Sparse Core Ops, SparseCore 0:
  28.8 32.9 reduce-scatter.15
  65.3 25.7 reduce-scatter.17
  93.5 34.9 all-gather.2
  137.5 17.3 reduce-scatter.11
  179.5 26.6 reduce-scatter.19
  208.4 34.9 all-gather.4
  252.6 17.3 reduce-scatter.13
where the time goes:
time: 342 us; the launch traced here: 341 us
  waiting for transfers between devices  141 us (41%)
  matrix products  89.7 us (26%)
  local copies, waits for them, and re-layouts  50.3 us (15%)
  blocking collectives  34.3 us (10%)
  between operations  14.3 us (4%)
  other arithmetic  6.53 us (2%)
  starting transfers between devices  5.43 us (2%)
    unnamed x10, waiting for transfers between devices  71 us
    all_gather x2, waiting for transfers between devices, layer_backward(): gathered = lax.all_gather(packed, 'row', axis=0, tiled=True)  51.3 us
    all_gather x3, blocking collectives, spread_panel(): return lax.all_gather(panel, 'col', axis=0, tiled=True)  34.3 us
    dot_general x2, matrix products, layer_backward(): lax.dot_general(x_whole, both_grads, CONTRACT_ROWS, preferred_element_typ...  31.1 us
    unnamed x19, local copies, waits for them, and re-layouts  30.7 us
    dot_general x2, matrix products, layer_backward(): lax.dot_general(hidden_whole, dy_whole, CONTRACT_ROWS, preferred_element_...  20.3 us
    broadcast_in_dim x1, local copies, waits for them, and re-layouts, shards(): both_total[:, hidden_width:][None]  19.6 us
    dot_general x2, matrix products, layer_backward(): lax.dot_general(both_grads, w_both, CONTRACT_COLS, preferred_element_type...  17.9 us
  transfers between devices with their start and end apart: 8, of which 7 were waited for; matrix products, arithmetic and copies ran while one was open for 31% of the time, Pallas kernels for 0%

commit v1 on v0

--- a/solution.py
+++ b/solution.py
@@ -1,6 +1,8 @@
 import jax
 import jax.numpy as jnp
 from jax import lax
+from jax.experimental import pallas as pl
+from jax.experimental.pallas import tpu as pltpu
 from jax.sharding import PartitionSpec as P
 
 CONTRACT_ROWS = (((0,), (0,)), ((), ()))
@@ -104,9 +106,330 @@
     )
 
 
+ORDER = pl.DeviceIdType.MESH
+
+
+def remote(src, dst, send_sem, recv_sem, target):
+    return pltpu.make_async_remote_copy(
+        src_ref=src, dst_ref=dst, send_sem=send_sem, recv_sem=recv_sem, device_id=target, device_id_type=ORDER
+    )
+
+
+def relay_kernel(
+    x_ref, top_ref, gate_ref, up_ref, down_ref,
+    grad_out, x_out, dy_out, packed_out,
+    w_gate, w_up, w_down, x_slots, dy_slots, part_send, part_recv, spread, gate_sum, up_sum,
+    branch, branch_send, branch_recv, result,
+    w_sem, x_send_sem, x_recv_sem, dy_send_sem, dy_recv_sem, part_send_sem, part_recv_sem,
+    spread_send_sem, spread_recv_sem, branch_send_sem, branch_recv_sem, out_sem, go_sem,
+):
+    section = lax.axis_index("section")
+    row = lax.axis_index("row")
+    col = lax.axis_index("col")
+    rows, width = part_send.shape[2], part_send.shape[3]
+    group = x_slots.shape[1]
+    is_top = section == 1
+    is_bottom = section == 0
+
+    def row_peer(d):
+        hi, lo = row // 2, row % 2
+        return ((hi + d // 2) % 2) * 2 + (lo + d % 2) % 2
+
+    def ahead(d):
+        return (col + d) % 4
+
+    def behind(d):
+        return (col + 4 - d) % 4
+
+    def weight_copy(a, d):
+        cols = pl.ds(pl.multiple_of(row_peer(d) * width, width), width)
+        if a == 2:
+            return pltpu.make_async_copy(down_ref.at[cols, :], w_down.at[d], w_sem.at[2, d])
+        source, target = ((gate_ref, w_gate), (up_ref, w_up))[a]
+        return pltpu.make_async_copy(source.at[:, cols], target.at[d], w_sem.at[a, d])
+
+    def x_copy(d):
+        return remote(x_ref, x_slots.at[d], x_send_sem.at[d], x_recv_sem.at[d], (section, row, ahead(d)))
+
+    def dy_copy(d):
+        return remote(top_ref, dy_slots.at[d], dy_send_sem.at[d], dy_recv_sem.at[d], (section, row, ahead(d)))
+
+    def pass_copy(d):
+        return remote(result, dy_slots.at[d], dy_send_sem.at[d], dy_recv_sem.at[d], (0, row, ahead(d)))
+
+    def part_copy(a, d):
+        return remote(
+            part_send.at[a, d], part_recv.at[a, d], part_send_sem.at[a, d], part_recv_sem.at[a, d],
+            (section, row_peer(d), col),
+        )
+
+    def spread_copy(a, d):
+        return remote(
+            spread.at[a, 0], spread.at[a, d], spread_send_sem.at[a, d], spread_recv_sem.at[a, d],
+            (section, row_peer(d), col),
+        )
+
+    def branch_copy(d):
+        return remote(
+            branch_send.at[d], branch_recv.at[d], branch_send_sem.at[d], branch_recv_sem.at[d],
+            (section, row, behind(d)),
+        )
+
+    def merge(slots, whole):
+        for d in range(4):
+            branch[d * group:(d + 1) * group, :] = slots[d].astype(jnp.float32)
+        whole[...] = branch[...].astype(jnp.bfloat16)
+
+    for d in (1, 2, 3):
+        x_copy(d).start()
+    x_slots[0] = x_ref[...]
+
+    @pl.when(is_top)
+    def _():
+        for d in (1, 2, 3):
+            dy_copy(d).start()
+        dy_slots[0] = top_ref[...]
+        for d in (3, 2, 1, 0):
+            weight_copy(2, d).start()
+
+    for d in (3, 2, 1, 0):
+        weight_copy(0, d).start()
+        weight_copy(1, d).start()
+
+    @pl.when(is_bottom)
+    def _():
+        for d in (3, 2, 1, 0):
+            weight_copy(2, d).start()
+
+    def hidden_terms():
+        merge(dy_slots, dy_out)
+
+        def step(i, carry):
+            d = 3 - i
+            weight_copy(2, d).wait()
+            part_send[2, d] = lax.dot_general(
+                dy_out[...], w_down[d], CONTRACT_COLS, preferred_element_type=jnp.float32
+            ).astype(jnp.bfloat16)
+
+            @pl.when(d > 0)
+            def _():
+                part_copy(2, d).start()
+            return carry
+
+        lax.fori_loop(0, 4, step, 0)
+
+    @pl.when(is_top)
+    def _():
+        for d in (1, 2, 3):
+            dy_copy(d).wait_recv()
+        hidden_terms()
+
+    for d in (1, 2, 3):
+        x_copy(d).wait_recv()
+    merge(x_slots, x_out)
+
+    def forward_step(i, carry):
+        d = 3 - i
+        weight_copy(0, d).wait()
+        weight_copy(1, d).wait()
+        for a, weight in enumerate((w_gate, w_up)):
+            part_send[a, d] = jnp.dot(
+                x_out[...], weight[d], preferred_element_type=jnp.float32
+            ).astype(jnp.bfloat16)
+
+            @pl.when(jnp.logical_and(is_top, d > 0))
+            def _():
+                part_copy(a, d).start()
+        return carry
+
+    lax.fori_loop(0, 4, forward_step, 0)
+
+    @pl.when(is_bottom)
+    def _():
+        pl.semaphore_wait(go_sem, 1)
+        for d in (3, 2, 1):
+            for a in range(2):
+                part_copy(a, d).start()
+
+    def summed(a, span):
+        total = part_send[a, 0, span, :].astype(jnp.float32)
+        for d in (1, 2, 3):
+            total = total + part_recv[a, d, span, :].astype(jnp.float32)
+        return total
+
+    def span_of(i):
+        return pl.ds(pl.multiple_of(i * 16, 16), 16)
+
+    for a in range(2):
+        for d in (1, 2, 3):
+            part_copy(a, d).wait_recv()
+
+    def hidden_step(i, carry):
+        span = span_of(i)
+        gate, up = summed(0, span), summed(1, span)
+        gate_sum[span, :] = gate
+        up_sum[span, :] = up
+        spread[0, 0, span, :] = (gate * jax.nn.sigmoid(gate) * up).astype(jnp.bfloat16)
+        return carry
+
+    lax.fori_loop(0, rows // 16, hidden_step, 0)
+
+    @pl.when(is_bottom)
+    def _():
+        for d in (3, 2, 1):
+            spread_copy(0, d).start()
+        for d in range(4):
+            pass_copy(d).wait_recv()
+        hidden_terms()
+
+    for d in (1, 2, 3):
+        part_copy(2, d).wait_recv()
+
+    def grad_step(i, carry):
+        span = span_of(i)
+        hidden_grad = summed(2, span)
+        gate, up = gate_sum[span, :], up_sum[span, :]
+        sigmoid_gate = jax.nn.sigmoid(gate)
+        slope = sigmoid_gate * (1.0 + gate * (1.0 - sigmoid_gate))
+        spread[1, 0, span, :] = (hidden_grad * up * slope).astype(jnp.bfloat16)
+        spread[2, 0, span, :] = (hidden_grad * (gate * sigmoid_gate)).astype(jnp.bfloat16)
+        return carry
+
+    lax.fori_loop(0, rows // 16, grad_step, 0)
+    for d in (3, 2, 1):
+        for a in (1, 2):
+            spread_copy(a, d).start()
+
+    branch[...] = jnp.zeros_like(branch)
+
+    def branch_step(d, carry):
+        @pl.when(d > 0)
+        def _():
+            spread_copy(1, d).wait_recv()
+            spread_copy(2, d).wait_recv()
+
+        branch[...] += lax.dot_general(
+            spread[1, d], w_gate[d], CONTRACT_COLS, preferred_element_type=jnp.float32
+        ) + lax.dot_general(
+            spread[2, d], w_up[d], CONTRACT_COLS, preferred_element_type=jnp.float32
+        )
+        return carry
+
+    lax.fori_loop(0, 4, branch_step, 0)
+    for d in (3, 2, 1, 0):
+        branch_send[d] = branch[d * group:(d + 1) * group, :].astype(jnp.bfloat16)
+        if d:
+            branch_copy(d).start()
+
+    @pl.when(is_top)
+    def _():
+        pl.semaphore_signal(go_sem, inc=1, device_id=(0, row, col), device_id_type=ORDER)
+        for d in (3, 2, 1):
+            spread_copy(0, d).start()
+
+    total = branch_send[0].astype(jnp.float32)
+    for d in (1, 2, 3):
+        branch_copy(d).wait_recv()
+        total = total + branch_recv[d].astype(jnp.float32)
+    result[...] = (dy_slots[0].astype(jnp.float32) + total).astype(jnp.bfloat16)
+
+    @pl.when(is_top)
+    def _():
+        for d in (3, 2, 1, 0):
+            pass_copy(d).start()
+
+    grad_out[...] = result[...]
+    for d in (1, 2, 3):
+        spread_copy(0, d).wait_recv()
+
+    def store_copy(a, d):
+        cols = pl.ds(pl.multiple_of(row_peer(d) * width, width), width)
+        return pltpu.make_async_copy(spread.at[a, d], packed_out.at[a, :, cols], out_sem.at[a, d])
+
+    for a in range(3):
+        for d in range(4):
+            store_copy(a, d).start()
+    for a in range(3):
+        for d in range(4):
+            store_copy(a, d).wait()
+    for d in (1, 2, 3):
+        x_copy(d).wait_send()
+        branch_copy(d).wait_send()
+        for a in range(3):
+            part_copy(a, d).wait_send()
+            spread_copy(a, d).wait_send()
+
+    @pl.when(is_top)
+    def _():
+        for d in (1, 2, 3):
+            dy_copy(d).wait_send()
+        for d in range(4):
+            pass_copy(d).wait_send()
+
+
+def fast_shards(section_inputs, out_grad, gate_weight, up_weight, down_weight):
+    panels = section_inputs[0]
+    micro, local, width = panels.shape
+    group = micro * local
+    rows = group * lax.axis_size("col")
+    hidden_width = gate_weight.shape[2]
+    piece = hidden_width // lax.axis_size("row")
+    vmem = pl.BlockSpec(memory_space=pltpu.VMEM)
+    anywhere = pl.BlockSpec(memory_space=pl.ANY)
+    bf16, f32 = jnp.bfloat16, jnp.float32
+    dma = pltpu.SemaphoreType.DMA
+    grad, x_whole, dy_whole, packed = pl.pallas_call(
+        relay_kernel,
+        out_shape=(
+            jax.ShapeDtypeStruct((group, width), bf16),
+            jax.ShapeDtypeStruct((rows, width), bf16),
+            jax.ShapeDtypeStruct((rows, width), bf16),
+            jax.ShapeDtypeStruct((3, rows, hidden_width), bf16),
+        ),
+        in_specs=[vmem, vmem, anywhere, anywhere, anywhere],
+        out_specs=(vmem, vmem, vmem, anywhere),
+        scratch_shapes=[
+            pltpu.VMEM((4, width, piece), bf16),
+            pltpu.VMEM((4, width, piece), bf16),
+            pltpu.VMEM((4, piece, width), bf16),
+            pltpu.VMEM((4, group, width), bf16),
+            pltpu.VMEM((4, group, width), bf16),
+            pltpu.VMEM((3, 4, rows, piece), bf16),
+            pltpu.VMEM((3, 4, rows, piece), bf16),
+            pltpu.VMEM((3, 4, rows, piece), bf16),
+            pltpu.VMEM((rows, piece), f32),
+            pltpu.VMEM((rows, piece), f32),
+            pltpu.VMEM((rows, width), f32),
+            pltpu.VMEM((4, group, width), bf16),
+            pltpu.VMEM((4, group, width), bf16),
+            pltpu.VMEM((group, width), bf16),
+            dma((3, 4)), dma((4,)), dma((4,)), dma((4,)), dma((4,)),
+            dma((3, 4)), dma((3, 4)), dma((3, 4)), dma((3, 4)), dma((4,)), dma((4,)),
+            dma((3, 4)), pltpu.SemaphoreType.REGULAR,
+        ],
+        compiler_params=pltpu.CompilerParams(has_side_effects=True, vmem_limit_bytes=56 * 2**20),
+    )(
+        panels.reshape(group, width), out_grad.reshape(group, width),
+        gate_weight[0], up_weight[0], down_weight[0],
+    )
+    grads = [
+        lax.dot_general(left, right, CONTRACT_ROWS, preferred_element_type=f32)
+        for left, right in ((x_whole, packed[1]), (x_whole, packed[2]), (packed[0], dy_whole))
+    ]
+    return (grad.reshape(panels.shape)[None], *(g[None] for g in grads))
+
+
+def fits_kernel(mesh, gate_weight, section_inputs):
+    sizes = mesh.shape
+    if (sizes["section"], sizes["row"], sizes["col"]) != (2, 4, 4):
+        return False
+    piece = gate_weight.shape[2] // (sizes["row"] * sizes["col"])
+    local = section_inputs.shape[1] * section_inputs.shape[2] // sizes["col"]
+    return piece % 128 == 0 and local % 8 == 0 and (local * sizes["col"]) % 16 == 0
+
+
 def solution(mesh):
-    return jax.shard_map(
-        shards,
+    specs = dict(
         mesh=mesh,
         in_specs=(
             P("section", None, "col", "row"),
@@ -123,3 +446,9 @@
         ),
         check_vma=False,
     )
+
+    def run(section_inputs, out_grad, gate_weight, up_weight, down_weight):
+        body = fast_shards if fits_kernel(mesh, gate_weight, section_inputs) else shards
+        return jax.shard_map(body, **specs)(section_inputs, out_grad, gate_weight, up_weight, down_weight)
+
+    return run

time: 342 us -> 119 us (0.35)
  the two profiles are of different devices: /device:TPU:1 before, /device:TPU:0 now
where the time goes in v1:
time: 119 us
  Pallas kernels  89.6 us (75%)
  matrix products  24 us (20%)
  local copies, waits for them, and re-layouts  4.38 us (4%)
    pallas_call x1, Pallas kernels, fast_shards(): pl.pallas_call(relay_kernel, out_shape=(jax.ShapeDtypeStruct((group, widt...  89.6 us
    dot_general x3, matrix products, fast_shards(): lax.dot_general(left, right, CONTRACT_ROWS, preferred_element_type=f32)  24 us

profile of v1, /device:TPU:0, one launch (start us, length us, event | category | flops | bytes accessed | tf_op | source)
XLA Modules:
  0.0 118.6 jit_solution(4246873074657181253)
XLA Ops:
  0.6 0.8 copy.12
  1.4 0.6 reshape_squeeze.3.x_ref
  2.1 0.8 copy.13
  2.9 0.6 reshape.11.top_ref
  3.5 89.6 %shard_map.84 = (bf16[24,1024]{1,0:T(8,128)(2,1)}, bf16[96,1024]{1,0:T(8,128)(2,1)}, bf16[96,1024]{1,0:T(8,128)(2,1)}, bf16[3,96,3584]{2,1,0:T(8,128)(2,1)}) custom-call(bf16[24,1024]{1,0:T(8,128)(2,1)} %reshape_squeeze.3.x_ref, bf16[24,1024]{1,0:T(8,128)(2,1)} %reshape.11.top_ref, bf16[1024,3584]{1,0:T(8,128)(2,1)} %bitcast.21, ...), custom_call_target="tpu_custom_call" | custom-call | tf_op jit(solution)/shard_map/pallas_call | solution.py:381
  93.1 0.8 broadcast_in_dim_reshape.3
  94.0 0.7 copy.14
  94.6 0.0 copy-start
  94.6 0.0 copy-start.1
  94.6 8.8 %convolution_bitcast_fusion = f32[1,3584,1024]{2,1,0:T(8,128)} fusion(bf16[96,1024]{1,0:T(8,128)(2,1)} %get-tuple-element.11, bf16[3,96,3584]{2,1,0:T(8,128)(2,1)} %get-tuple-element.10), kind=kOutput, calls=%fused_computation | convolution fusion | flops 704643072 | bytes 15564800 | tf_op jit(solution)/shard_map/dot_general | solution.py:416
  103.5 0.0 copy-done
  103.5 0.0 copy-done.1
  103.5 7.6 %convolution_bitcast_fusion.1 = f32[1,1024,3584]{2,1,0:T(8,128)} fusion(bf16[96,1024]{1,0:T(8,128)(2,1)S(1)} %copy-done.1, bf16[3,96,3584]{2,1,0:T(8,128)(2,1)S(1)} %copy-done), kind=kOutput, calls=%fused_computation.1 | convolution fusion | flops 704643072 | bytes 15564800 | tf_op jit(solution)/shard_map/dot_general | solution.py:416
  111.0 7.6 %convolution_bitcast_fusion.2 = f32[1,1024,3584]{2,1,0:T(8,128)} fusion(bf16[96,1024]{1,0:T(8,128)(2,1)S(1)} %copy-done.1, bf16[3,96,3584]{2,1,0:T(8,128)(2,1)S(1)} %copy-done), kind=kOutput, calls=%fused_computation.2 | convolution fusion | flops 704643072 | bytes 15564800 | tf_op jit(solution)/shard_map/dot_general | solution.py:416
Async XLA Ops:
  94.6 8.9 %copy-start = (bf16[3,96,3584]{2,1,0:T(8,128)(2,1)S(1)}, bf16[3,96,3584]{2,1,0:T(8,128)(2,1)}, u32[]{:S(2)}) copy-start(bf16[3,96,3584]{2,1,0:T(8,128)(2,1)} %get-tuple-element.10) | copy-start | bytes 6193156
  94.6 8.9 %copy-start.1 = (bf16[96,1024]{1,0:T(8,128)(2,1)S(1)}, bf16[96,1024]{1,0:T(8,128)(2,1)}, u32[]{:S(2)}) copy-start(bf16[96,1024]{1,0:T(8,128)(2,1)} %get-tuple-element.9) | copy-start | bytes 589828

commit v2 on v1

--- a/solution.py
+++ b/solution.py
@@ -121,13 +121,14 @@
     w_gate, w_up, w_down, x_slots, dy_slots, part_send, part_recv, spread, gate_sum, up_sum,
     branch, branch_send, branch_recv, result,
     w_sem, x_send_sem, x_recv_sem, dy_send_sem, dy_recv_sem, part_send_sem, part_recv_sem,
-    spread_send_sem, spread_recv_sem, branch_send_sem, branch_recv_sem, out_sem, go_sem,
+    spread_send_sem, spread_recv_sem, branch_send_sem, branch_recv_sem, onward_send_sem, onward_recv_sem, out_sem, go_sem,
 ):
     section = lax.axis_index("section")
     row = lax.axis_index("row")
     col = lax.axis_index("col")
     rows, width = part_send.shape[2], part_send.shape[3]
-    group = x_slots.shape[1]
+    local, micro = x_slots.shape[1:3]
+    group = local * micro
     is_top = section == 1
     is_bottom = section == 0
 
@@ -157,17 +158,35 @@
     def pass_copy(d):
         return remote(result, dy_slots.at[d], dy_send_sem.at[d], dy_recv_sem.at[d], (0, row, ahead(d)))
 
-    def part_copy(a, d):
+    def half(h):
+        return pl.ds(h * (rows // 2), rows // 2)
+
+    def part_copy(a, d, h):
         return remote(
-            part_send.at[a, d], part_recv.at[a, d], part_send_sem.at[a, d], part_recv_sem.at[a, d],
-            (section, row_peer(d), col),
+            part_send.at[a, d, half(h), :], part_recv.at[a, d, half(h), :],
+            part_send_sem.at[a, d, h], part_recv_sem.at[a, d, h], (section, row_peer(d), col),
         )
 
-    def spread_copy(a, d):
+    def spread_copy(a, d, h):
         return remote(
-            spread.at[a, 0], spread.at[a, d], spread_send_sem.at[a, d], spread_recv_sem.at[a, d],
-            (section, row_peer(d), col),
+            spread.at[a, 0, half(h), :], spread.at[a, d, half(h), :],
+            spread_send_sem.at[a, d, h], spread_recv_sem.at[a, d, h], (section, row_peer(d), col),
         )
+
+    def onward_copy(a, d):
+        return remote(
+            spread.at[a, d, half(d - 1), :], spread.at[a, 3, half(d - 1), :],
+            onward_send_sem.at[a, d], onward_recv_sem.at[a, d], (section, row_peer(3 - d), col),
+        )
+
+    def relay(*arrays):
+        for d in (1, 2):
+            for a in arrays:
+                spread_copy(a, d, d - 1).wait_recv()
+                onward_copy(a, d).start()
+        for d in (1, 2):
+            for a in arrays:
+                spread_copy(a, d, 2 - d).wait_recv()
 
     def branch_copy(d):
         return remote(
@@ -177,29 +196,34 @@
 
     def merge(slots, whole):
         for d in range(4):
-            branch[d * group:(d + 1) * group, :] = slots[d].astype(jnp.float32)
+            for t in range(local):
+                first = d * group + t * micro
+                branch[first:first + micro, :] = slots[d, t].astype(jnp.float32)
         whole[...] = branch[...].astype(jnp.bfloat16)
-
-    for d in (1, 2, 3):
-        x_copy(d).start()
-    x_slots[0] = x_ref[...]
-
-    @pl.when(is_top)
-    def _():
-        for d in (1, 2, 3):
-            dy_copy(d).start()
-        dy_slots[0] = top_ref[...]
-        for d in (3, 2, 1, 0):
-            weight_copy(2, d).start()
 
     for d in (3, 2, 1, 0):
         weight_copy(0, d).start()
         weight_copy(1, d).start()
-
-    @pl.when(is_bottom)
-    def _():
-        for d in (3, 2, 1, 0):
-            weight_copy(2, d).start()
+    for d in (3, 2, 1, 0):
+        weight_copy(2, d).start()
+
+    barrier = pltpu.get_barrier_semaphore()
+    greeted = [(section, row, ahead(d)) for d in (1, 2, 3)]
+    greeted += [(section, row_peer(d), col) for d in (1, 2, 3)]
+    greeted += [(1 - section, row, ahead(d)) for d in range(4)]
+    for device in greeted:
+        pl.semaphore_signal(barrier, inc=1, device_id=device, device_id_type=ORDER)
+    pl.semaphore_wait(barrier, len(greeted))
+
+    for d in (2, 1, 3):
+        x_copy(d).start()
+    x_slots[0] = x_ref[...]
+
+    @pl.when(is_top)
+    def _():
+        for d in (2, 1, 3):
+            dy_copy(d).start()
+        dy_slots[0] = top_ref[...]
 
     def hidden_terms():
         merge(dy_slots, dy_out)
@@ -213,16 +237,10 @@
 
             @pl.when(d > 0)
             def _():
-                part_copy(2, d).start()
+                part_copy(2, d, 0).start()
             return carry
 
         lax.fori_loop(0, 4, step, 0)
-
-    @pl.when(is_top)
-    def _():
-        for d in (1, 2, 3):
-            dy_copy(d).wait_recv()
-        hidden_terms()
 
     for d in (1, 2, 3):
         x_copy(d).wait_recv()
@@ -239,7 +257,7 @@
 
             @pl.when(jnp.logical_and(is_top, d > 0))
             def _():
-                part_copy(a, d).start()
+                part_copy(a, d, 0).start()
         return carry
 
     lax.fori_loop(0, 4, forward_step, 0)
@@ -247,9 +265,28 @@
     @pl.when(is_bottom)
     def _():
         pl.semaphore_wait(go_sem, 1)
+        for h in range(2):
+            for d in (3, 2, 1):
+                for a in range(2):
+                    part_copy(a, d, h).start()
+        for d in range(4):
+            pass_copy(d).wait_recv()
+
+    @pl.when(is_top)
+    def _():
+        for d in (1, 2, 3):
+            dy_copy(d).wait_recv()
+
+    hidden_terms()
+
+    @pl.when(is_top)
+    def _():
         for d in (3, 2, 1):
             for a in range(2):
-                part_copy(a, d).start()
+                part_copy(a, d, 1).start()
+
+    for d in (3, 2, 1):
+        part_copy(2, d, 1).start()
 
     def summed(a, span):
         total = part_send[a, 0, span, :].astype(jnp.float32)
@@ -259,10 +296,6 @@
 
     def span_of(i):
         return pl.ds(pl.multiple_of(i * 16, 16), 16)
-
-    for a in range(2):
-        for d in (1, 2, 3):
-            part_copy(a, d).wait_recv()
 
     def hidden_step(i, carry):
         span = span_of(i)
@@ -271,19 +304,6 @@
         up_sum[span, :] = up
         spread[0, 0, span, :] = (gate * jax.nn.sigmoid(gate) * up).astype(jnp.bfloat16)
         return carry
-
-    lax.fori_loop(0, rows // 16, hidden_step, 0)
-
-    @pl.when(is_bottom)
-    def _():
-        for d in (3, 2, 1):
-            spread_copy(0, d).start()
-        for d in range(4):
-            pass_copy(d).wait_recv()
-        hidden_terms()
-
-    for d in (1, 2, 3):
-        part_copy(2, d).wait_recv()
 
     def grad_step(i, carry):
         span = span_of(i)
@@ -295,18 +315,41 @@
         spread[2, 0, span, :] = (hidden_grad * (gate * sigmoid_gate)).astype(jnp.bfloat16)
         return carry
 
-    lax.fori_loop(0, rows // 16, grad_step, 0)
-    for d in (3, 2, 1):
+    steps = rows // 32
+    for h in range(2):
+        for a in range(2):
+            for d in (1, 2, 3):
+                part_copy(a, d, h).wait_recv()
+        lax.fori_loop(h * steps, (h + 1) * steps, hidden_step, 0)
+        for d in (1, 2, 3):
+            part_copy(2, d, h).wait_recv()
+        lax.fori_loop(h * steps, (h + 1) * steps, grad_step, 0)
         for a in (1, 2):
-            spread_copy(a, d).start()
+            for d in (1, 2):
+                spread_copy(a, d, h).start()
+
+    @pl.when(is_bottom)
+    def _():
+        for h in range(2):
+            for d in (1, 2):
+                spread_copy(0, d, h).start()
+
+    def partner_go():
+        pl.semaphore_signal(go_sem, inc=1, device_id=(1 - section, row, col), device_id_type=ORDER)
 
     branch[...] = jnp.zeros_like(branch)
 
     def branch_step(d, carry):
-        @pl.when(d > 0)
+        @pl.when(d == 1)
         def _():
-            spread_copy(1, d).wait_recv()
-            spread_copy(2, d).wait_recv()
+            relay(1, 2)
+
+        @pl.when(d == 3)
+        def _():
+            for a in (1, 2):
+                for e in (1, 2):
+                    onward_copy(a, e).wait_recv()
+            partner_go()
 
         branch[...] += lax.dot_general(
             spread[1, d], w_gate[d], CONTRACT_COLS, preferred_element_type=jnp.float32
@@ -316,39 +359,42 @@
         return carry
 
     lax.fori_loop(0, 4, branch_step, 0)
-    for d in (3, 2, 1, 0):
+    for d in (2, 3, 1, 0):
         branch_send[d] = branch[d * group:(d + 1) * group, :].astype(jnp.bfloat16)
         if d:
             branch_copy(d).start()
 
-    @pl.when(is_top)
-    def _():
-        pl.semaphore_signal(go_sem, inc=1, device_id=(0, row, col), device_id_type=ORDER)
-        for d in (3, 2, 1):
-            spread_copy(0, d).start()
-
-    total = branch_send[0].astype(jnp.float32)
+    def store_copy(a, d):
+        cols = pl.ds(pl.multiple_of(row_peer(d) * width, width), width)
+        return pltpu.make_async_copy(spread.at[a, d], packed_out.at[a, :, cols], out_sem.at[a, d])
+
+    for a in (1, 2):
+        for d in range(4):
+            store_copy(a, d).start()
+
+    total = dy_out[:group, :].astype(jnp.float32) + branch_send[0].astype(jnp.float32)
     for d in (1, 2, 3):
         branch_copy(d).wait_recv()
         total = total + branch_recv[d].astype(jnp.float32)
-    result[...] = (dy_slots[0].astype(jnp.float32) + total).astype(jnp.bfloat16)
+    branch[:group, :] = total
+    for t in range(local):
+        result[t] = branch[t * micro:(t + 1) * micro, :].astype(jnp.bfloat16)
 
     @pl.when(is_top)
     def _():
-        for d in (3, 2, 1, 0):
+        for d in (2, 1, 3, 0):
             pass_copy(d).start()
+        pl.semaphore_wait(go_sem, 1)
+        for h in range(2):
+            for d in (1, 2):
+                spread_copy(0, d, h).start()
 
     grad_out[...] = result[...]
-    for d in (1, 2, 3):
-        spread_copy(0, d).wait_recv()
-
-    def store_copy(a, d):
-        cols = pl.ds(pl.multiple_of(row_peer(d) * width, width), width)
-        return pltpu.make_async_copy(spread.at[a, d], packed_out.at[a, :, cols], out_sem.at[a, d])
-
-    for a in range(3):
-        for d in range(4):
-            store_copy(a, d).start()
+    relay(0)
+    for d in (1, 2):
+        onward_copy(0, d).wait_recv()
+    for d in range(4):
+        store_copy(0, d).start()
     for a in range(3):
         for d in range(4):
             store_copy(a, d).wait()
@@ -356,8 +402,13 @@
         x_copy(d).wait_send()
         branch_copy(d).wait_send()
         for a in range(3):
-            part_copy(a, d).wait_send()
-            spread_copy(a, d).wait_send()
+            for h in range(2):
+                part_copy(a, d, h).wait_send()
+    for d in (1, 2):
+        for a in range(3):
+            for h in range(2):
+                spread_copy(a, d, h).wait_send()
+            onward_copy(a, d).wait_send()
 
     @pl.when(is_top)
     def _():
@@ -367,10 +418,41 @@
             pass_copy(d).wait_send()
 
 
+def update_kernel(x_ref, dy_ref, packed_ref, gate_out, up_out, down_out):
+    for left, right, out in (
+        (x_ref[...], packed_ref[1], gate_out),
+        (x_ref[...], packed_ref[2], up_out),
+        (packed_ref[0], dy_ref[...], down_out),
+    ):
+        out[...] = lax.dot_general(left, right, CONTRACT_ROWS, preferred_element_type=jnp.float32)
+
+
+def weight_updates(x_whole, dy_whole, packed):
+    rows, width = x_whole.shape
+    hidden_width = packed.shape[2]
+    tile = next(t for t in (512, 256, 128) if hidden_width % t == 0)
+    f32 = jnp.float32
+    whole = pl.BlockSpec((rows, width), lambda j: (0, 0))
+    wide = pl.BlockSpec((width, tile), lambda j: (0, j))
+    return pl.pallas_call(
+        update_kernel,
+        grid=(hidden_width // tile,),
+        out_shape=(
+            jax.ShapeDtypeStruct((width, hidden_width), f32),
+            jax.ShapeDtypeStruct((width, hidden_width), f32),
+            jax.ShapeDtypeStruct((hidden_width, width), f32),
+        ),
+        in_specs=[whole, whole, pl.BlockSpec((3, rows, tile), lambda j: (0, 0, j))],
+        out_specs=(wide, wide, pl.BlockSpec((tile, width), lambda j: (j, 0))),
+        compiler_params=pltpu.CompilerParams(vmem_limit_bytes=60 * 2**20),
+    )(x_whole, dy_whole, packed)
+
+
 def fast_shards(section_inputs, out_grad, gate_weight, up_weight, down_weight):
     panels = section_inputs[0]
     micro, local, width = panels.shape
     group = micro * local
+    held = (local, micro, width)
     rows = group * lax.axis_size("col")
     hidden_width = gate_weight.shape[2]
     piece = hidden_width // lax.axis_size("row")
@@ -381,7 +463,7 @@
     grad, x_whole, dy_whole, packed = pl.pallas_call(
         relay_kernel,
         out_shape=(
-            jax.ShapeDtypeStruct((group, width), bf16),
+            jax.ShapeDtypeStruct(held, bf16),
             jax.ShapeDtypeStruct((rows, width), bf16),
             jax.ShapeDtypeStruct((rows, width), bf16),
             jax.ShapeDtypeStruct((3, rows, hidden_width), bf16),
@@ -392,8 +474,8 @@
             pltpu.VMEM((4, width, piece), bf16),
             pltpu.VMEM((4, width, piece), bf16),
             pltpu.VMEM((4, piece, width), bf16),
-            pltpu.VMEM((4, group, width), bf16),
-            pltpu.VMEM((4, group, width), bf16),
+            pltpu.VMEM((4, *held), bf16),
+            pltpu.VMEM((4, *held), bf16),
             pltpu.VMEM((3, 4, rows, piece), bf16),
             pltpu.VMEM((3, 4, rows, piece), bf16),
             pltpu.VMEM((3, 4, rows, piece), bf16),
@@ -402,21 +484,19 @@
             pltpu.VMEM((rows, width), f32),
             pltpu.VMEM((4, group, width), bf16),
             pltpu.VMEM((4, group, width), bf16),
-            pltpu.VMEM((group, width), bf16),
+            pltpu.VMEM(held, bf16),
             dma((3, 4)), dma((4,)), dma((4,)), dma((4,)), dma((4,)),
-            dma((3, 4)), dma((3, 4)), dma((3, 4)), dma((3, 4)), dma((4,)), dma((4,)),
-            dma((3, 4)), pltpu.SemaphoreType.REGULAR,
+            *[dma((3, 4, 2))] * 4, dma((4,)), dma((4,)),
+            dma((3, 4)), dma((3, 4)), dma((3, 4)), pltpu.SemaphoreType.REGULAR,
         ],
-        compiler_params=pltpu.CompilerParams(has_side_effects=True, vmem_limit_bytes=56 * 2**20),
+        compiler_params=pltpu.CompilerParams(collective_id=0, has_side_effects=True, vmem_limit_bytes=56 * 2**20),
     )(
-        panels.reshape(group, width), out_grad.reshape(group, width),
+        panels.transpose(1, 0, 2), out_grad.transpose(1, 0, 2),
         gate_weight[0], up_weight[0], down_weight[0],
     )
-    grads = [
-        lax.dot_general(left, right, CONTRACT_ROWS, preferred_element_type=f32)
-        for left, right in ((x_whole, packed[1]), (x_whole, packed[2]), (packed[0], dy_whole))
-    ]
-    return (grad.reshape(panels.shape)[None], *(g[None] for g in grads))
+    grads = weight_updates(x_whole, dy_whole, packed)
+    grad = grad.transpose(1, 0, 2)
+    return (grad[None], *(g[None] for g in grads))
 
 
 def fits_kernel(mesh, gate_weight, section_inputs):
@@ -425,7 +505,7 @@
         return False
     piece = gate_weight.shape[2] // (sizes["row"] * sizes["col"])
     local = section_inputs.shape[1] * section_inputs.shape[2] // sizes["col"]
-    return piece % 128 == 0 and local % 8 == 0 and (local * sizes["col"]) % 16 == 0
+    return piece % 128 == 0 and local % 8 == 0 and (local * sizes["col"]) % 32 == 0
 
 
 def solution(mesh):

time: 119 us -> 88.3 us (0.74)
  matrix products: 24 us -> 0 us
  Pallas kernels: 89.6 us -> 86 us
  local copies, waits for them, and re-layouts: 4.38 us -> 1.45 us
    dot_general x3 -> x0, matrix products: 24 us -> none  [fast_shards(): lax.dot_general(left, right, CONTRACT_ROWS, preferred_element_type=f32)]
    pallas_call x1 -> x2, Pallas kernels: 89.6 us -> 86 us  [the longest x1 70.3 us: fast_shards(): pl.pallas_call(relay_kernel, out_shape=(jax.ShapeDtypeStruct(held, bf16),...]
    another operation x2 -> x0, local copies, waits for them, and re-layouts: 1.45 us -> none  [the longest x1 0.81 us: fast_shards(): return (grad.reshape(panels.shape)[None], *(g[None] for g in grads))]
where the time goes in v2:
time: 88.3 us; the launch traced here: 88.1 us
  Pallas kernels  86 us (97%)
  local copies, waits for them, and re-layouts  1.45 us (2%)
    pallas_call x1, Pallas kernels, fast_shards(): pl.pallas_call(relay_kernel, out_shape=(jax.ShapeDtypeStruct(held, bf16),...  70.3 us
    pallas_call x1, Pallas kernels, weight_updates(): pl.pallas_call(update_kernel, grid=(hidden_width // tile,), out_shape=(ja...  15.6 us

profile of v2, /device:TPU:0, one launch (start us, length us, event | category | flops | bytes accessed | tf_op | source)
XLA Modules:
  0.0 88.1 jit_solution(9547949476206491494)
XLA Ops:
  0.6 70.3 %shard_map.84 = (bf16[12,2,1024]{2,1,0:T(2,128)(2,1)}, bf16[96,1024]{1,0:T(8,128)(2,1)}, bf16[96,1024]{1,0:T(8,128)(2,1)}, bf16[3,96,3584]{2,1,0:T(8,128)(2,1)}) custom-call(bf16[12,2,1024]{2,1,0:T(2,128)(2,1)} %bitcast.17, bf16[12,2,1024]{2,1,0:T(2,128)(2,1)} %bitcast.18, bf16[1024,3584]{1,0:T(8,128)(2,1)} %bitcast.13, bf16[1024,3584]{1,0:T(8,128)(2,1)} %bitcast.14, ...), custom_call_target="tpu_custom_call" | custom-call | tf_op jit(solution)/shard_map/pallas_call | solution.py:463
  71.0 15.6 %shard_map.85 = (f32[1024,3584]{1,0:T(8,128)}, f32[1024,3584]{1,0:T(8,128)}, f32[3584,1024]{1,0:T(8,128)}) custom-call(bf16[96,1024]{1,0:T(8,128)(2,1)} %get-tuple-element.12.x_ref, bf16[96,1024]{1,0:T(8,128)(2,1)} %get-tuple-element.13.dy_ref, bf16[3,96,3584]{2,1,0:T(8,128)(2,1)} %get-tuple-element.14.packed_ref), custom_call_target="tpu_custom_call" | custom-call | tf_op jit(solution)/shard_map/pallas_call | solution.py:437
  86.6 1.5 %copy.10 = bf16[1,2,12,1024]{3,1,2,0:T(2,128)(2,1)} copy(bf16[1,2,12,1024]{3,1,2,0:T(2,128)(2,1)} %bitcast.16) | data formatting | bytes 98304
